TPU v7x, 32 devices: a whole 2x2x4 slice. The times are simulated.
32 devices in a mesh: ka: 8 (over z, y), ga: 4 (over x, core).
Axes of the slice: x: 2, y: 2, z: 4, core: 2. Of those that a mesh axis runs over, the one named last changes fastest.
Arguments:
- x_dens: bfloat16 [32, 64, 1500], P('ka', None, 'ga'), may hold values from -6 to 6
- y_dens: bfloat16 [32, 64, 1500], P('ka', None, 'ga'), may hold values from -0.15625 to 0.15625
- p_dens: bfloat16 [32, 64, 1500], P('ka', None, 'ga'), may hold values from -1 to 1
- coulomb: float32 [1500], P('ga'), may hold values from 0.1 to 2
- screened: bfloat16 [16, 1500, 1500], P('ka', 'ga'), may hold values from -0.15625 to 0.15625
- pairs: int32 [128, 3], P('ka'), may hold values from 0 to 31, as said below
- q_slot: int32 [16], replicated, may hold values from 0 to 15, as said below
Outputs:
- blocks: float32 [128, 4096], P('ka')
- mirrored: float32 [32, 4096], P('ka')
Inputs may be any that keep to these rules, and one draw needn't show every extreme that they name: `pairs`: column 0 of the rows held by index d of ka lies in d * 4 to (d + 1) * 4 - 1; column 1 is any k-point; column 2 is a momentum transfer below 16. Among one index's 16 rows at most 2 have a second k-point held by one same index, and this is reached; at most 2 have q_slot[q] // 2 equal to one same value, and this is reached. `q_slot`: A permutation of the slots; slot s of screened is held by index s // 2 of ka.
All inputs are finite; a program needn't handle non-finite values.
Results may differ from a plain program's by a relative error of at most 0.0014.
Values may be sent and summed in bfloat16 or wider, within the bound.
A program may use at most 192 MiB of HBM per device.

v0:
```python
import jax
import jax.numpy as jnp
from jax import lax
from jax.sharding import PartitionSpec as P

CAPQ = 2
CAPK = 2


def earlier_count(owners):
    places = jnp.arange(owners.shape[0])
    same_owner = owners[:, None] == owners[None, :]
    before = places[:, None] > places[None, :]
    return jnp.sum(jnp.logical_and(same_owner, before).astype(jnp.int32), axis=1)


def per_device(x_dens, y_dens, p_dens, coulomb, screened, pairs, q_slot):
    n_ka = lax.axis_size("ka")
    mine_index = lax.axis_index("ka")
    per_dev, transitions, g_local = x_dens.shape
    q_slots = screened.shape[0]
    pair_rows = pairs.shape[0]
    k_local = pairs[:, 0] - mine_index * per_dev
    partner = pairs[:, 1]
    q_index = pairs[:, 2]
    slot_of = jnp.sum(
        jnp.where(q_index[:, None] == jnp.arange(q_slot.shape[0])[None, :], q_slot[None, :], 0),
        axis=1,
    )
    q_owner = slot_of // q_slots
    q_local = slot_of % q_slots
    q_rank = earlier_count(q_owner)
    q_route = ((q_owner * CAPQ + q_rank)[:, None] == jnp.arange(n_ka * CAPQ)[None, :]).astype(
        jnp.bfloat16
    )
    pick_first = (k_local[:, None] == jnp.arange(per_dev)[None, :]).astype(jnp.bfloat16)
    x_rows = jnp.einsum(
        "jk,kig->jig", pick_first, x_dens, preferred_element_type=jnp.float32
    ).astype(jnp.bfloat16)
    p_rows = jnp.einsum(
        "jk,kig->jig", pick_first, p_dens, preferred_element_type=jnp.float32
    ).astype(jnp.bfloat16)
    send_x = jnp.einsum("js,jig->sig", q_route, x_rows, preferred_element_type=jnp.float32).astype(
        jnp.bfloat16
    )
    send_x = send_x.reshape(n_ka, CAPQ, transitions, g_local)
    send_q = jnp.sum(q_route.astype(jnp.int32) * q_local[:, None], axis=0).reshape(n_ka, CAPQ)
    got_x, got_q = (
        lax.all_to_all(send_x, "ka", split_axis=0, concat_axis=0, tiled=True),
        lax.all_to_all(send_q, "ka", split_axis=0, concat_axis=0, tiled=True),
    )
    chosen = (got_q[:, :, None] == jnp.arange(q_slots)[None, None, :]).astype(jnp.bfloat16)
    stacked = got_x[:, :, None, :, :] * chosen[:, :, :, None, None]
    partial_value = jnp.einsum(
        "ncsig,sgh->hnci", stacked, screened, preferred_element_type=jnp.float32
    )
    half_rows = lax.psum_scatter(
        partial_value.reshape(lax.axis_size("ga") * g_local, n_ka, CAPQ * transitions),
        "ga",
        scatter_dimension=0,
        tiled=True,
    ).astype(jnp.bfloat16)
    returned = lax.all_to_all(half_rows, "ka", split_axis=1, concat_axis=1, tiled=True)
    returned = returned.reshape(g_local, n_ka * CAPQ, transitions)
    u_rows = jnp.einsum(
        "js,gsi->jig", q_route, returned, preferred_element_type=jnp.float32
    ).astype(jnp.bfloat16)
    all_pairs = lax.all_gather(pairs, "ka", axis=0, tiled=True).reshape(n_ka, pair_rows, 3)
    seconds = all_pairs[:, :, 1]
    k_owners = seconds // per_dev
    k_ranks = jax.vmap(earlier_count)(k_owners)
    held_here = k_owners == mine_index
    rank_hot = (k_ranks[:, :, None] == jnp.arange(CAPK)[None, None, :]).astype(jnp.float32)
    local_hot = jnp.logical_and(
        (seconds - mine_index * per_dev)[:, :, None] == jnp.arange(per_dev)[None, None, :],
        held_here[:, :, None],
    ).astype(jnp.float32)
    selector = jnp.einsum("njc,njk->nck", rank_hot, local_hot).astype(jnp.bfloat16)
    send_y = jnp.einsum(
        "nck,kig->ncig", selector, y_dens, preferred_element_type=jnp.float32
    ).astype(jnp.bfloat16)
    send_p = jnp.einsum(
        "nck,kig->ncig", selector, p_dens, preferred_element_type=jnp.float32
    ).astype(jnp.bfloat16)
    got_y, got_p = (
        lax.all_to_all(send_y, "ka", split_axis=0, concat_axis=0, tiled=True),
        lax.all_to_all(send_p, "ka", split_axis=0, concat_axis=0, tiled=True),
    )
    own_rank = earlier_count(partner // per_dev)
    pick_second = (
        (partner // per_dev * CAPK + own_rank)[:, None] == jnp.arange(n_ka * CAPK)[None, :]
    ).astype(jnp.bfloat16)
    y_rows = jnp.einsum(
        "js,sig->jig",
        pick_second,
        got_y.reshape(n_ka * CAPK, transitions, g_local),
        preferred_element_type=jnp.float32,
    ).astype(jnp.bfloat16)
    pp_rows = jnp.einsum(
        "js,sig->jig",
        pick_second,
        got_p.reshape(n_ka * CAPK, transitions, g_local),
        preferred_element_type=jnp.float32,
    ).astype(jnp.bfloat16)
    direct = jnp.einsum("jig,jhg->jih", u_rows, y_rows, preferred_element_type=jnp.float32)
    weighted = p_rows.astype(jnp.float32) * coulomb[None, None, :]
    exchange_term = jnp.einsum(
        "jig,jhg->jih", weighted, pp_rows.astype(jnp.float32), precision=lax.Precision.HIGHEST
    )
    kernel_block = lax.psum(2.0 * exchange_term - direct, "ga")
    blocks = kernel_block.reshape(pair_rows, transitions * transitions)
    flipped = jnp.transpose(kernel_block, (0, 2, 1)).reshape(pair_rows, transitions * transitions)
    selector = (partner[:, None] == jnp.arange(lax.axis_size("ka") * per_dev)[None, :]).astype(
        jnp.float32
    )
    mirrored = lax.psum_scatter(
        jnp.dot(selector.T, flipped, precision=lax.Precision.HIGHEST),
        "ka",
        scatter_dimension=0,
        tiled=True,
    )
    return (blocks, mirrored)


def solution(mesh):
    in_specs = (
        P("ka", None, "ga"),
        P("ka", None, "ga"),
        P("ka", None, "ga"),
        P("ga"),
        P("ka", "ga", None),
        P("ka", None),
        P(),
    )
    out_specs = (P("ka", None), P("ka", None))
    return jax.shard_map(
        per_device, mesh=mesh, in_specs=in_specs, out_specs=out_specs, check_vma=False
    )
```

profile of v0, /device:TPU:0, one launch (start us, length us, event | category | flops | bytes accessed | tf_op | source)
XLA Modules:
  0.0 274.0 jit_solution(15575906817718074861)
XLA Ops:
  7.2 0.9 slice_bitcast_fusion.1
  8.1 0.8 select_reduce_fusion
  8.9 0.2 convert_reduce_fusion.1
  9.2 0.7 all_to_all.20
  9.9 7.3 %all-to-all-start.2 = ((s32[8,1,2]{2,1,0:T(1,128)}), s32[8,1,2]{2,1,0:T(1,128)S(1)}, u32[]{:S(2)}, u32[]{:S(2)}) async-start(s32[8,1,2]{2,1,0:T(1,128)} %bitcast.18), calls=%async_computation.2 | async-start | bytes 8192 | tf_op jit(solution)/shard_map/all_to_all | solution.py:50
  17.2 2.5 convolution_convert_fusion.3
  19.7 2.2 reshape.166
  21.9 1.5 copy.117
  23.4 0.2 all-to-all-done.2
  23.6 5.8 %all-to-all-start.1 = ((bf16[8,2,64,375]{3,1,2,0:T(2,128)(2,1)}), bf16[8,2,64,375]{3,1,2,0:T(2,128)(2,1)S(1)}, u32[]{:S(2)}, u32[]{:S(2)}) async-start(bf16[8,2,64,375]{3,1,2,0:T(2,128)(2,1)} %copy.117), calls=%async_computation.1 | async-start | bytes 1572864 | tf_op jit(solution)/shard_map/all_to_all | solution.py:49
  29.5 19.6 %all-to-all-done.1 = bf16[8,2,64,375]{3,1,2,0:T(2,128)(2,1)S(1)} async-done(((bf16[8,2,64,375]{3,1,2,0:T(2,128)(2,1)}), bf16[8,2,64,375]{3,1,2,0:T(2,128)(2,1)S(1)}, u32[]{:S(2)}, u32[]{:S(2)}) %all-to-all-start.1) | async-done | bytes 768032 | tf_op jit(solution)/shard_map/all_to_all | solution.py:49
  49.1 0.1 copy.118
  49.2 5.0 %fusion = f32[8,2,64,1500,1]{3,2,4,1,0:T(8,128)} fusion(bf16[2,375,1500,1,1]{2,0,1,4,3:T(2,128)(2,1)S(1)} %bitcast.72, bf16[8,2,2]{2,1,0:T(2,128)(2,1)S(1)} %compare_convert_fusion, bf16[8,2,64,375]{3,2,1,0:T(8,128)(2,1)S(1)} %copy.118), kind=kOutput, calls=%fused_computation | convolution fusion | flops 2304768000 | bytes 9162064 | tf_op jit(solution)/shard_map/ncsig,sgh->hnci/dot_general | solution.py:54
  54.2 6.5 %copy.123 = f32[1500,8,128]{2,1,0:T(8,128)} copy(f32[1500,8,128]{0,2,1:T(8,128)} %bitcast.73) | data formatting | bytes 12288000 | tf_op jit(solution)/shard_map/reshape | solution.py:58
  60.7 0.7 copy-done.6
  61.4 26.1 %all-gather = s32[8,16,3]{1,2,0:T(4,128)S(1)} all-gather(s32[1,16,3]{1,2,0:T(4,128)S(1)} %bitcast.81), channel_id=1, replica_groups=mesh['ka'=8,'ga'=4] {'ka'}, dimensions={0}, use_global_device_ids=true | all-gather | bytes 1728 | tf_op jit(solution)/shard_map/all_gather | solution.py:68
  87.5 0.3 convert_reduce_fusion
  88.1 0.4 convolution_convert_fusion.5
  88.5 1.0 copy.111
  89.6 3.5 %all-to-all-start = ((bf16[8,2,64,375]{3,2,1,0:T(8,128)(2,1)}), bf16[8,2,64,375]{3,2,1,0:T(8,128)(2,1)S(1)}, u32[]{:S(2)}, u32[]{:S(2)}) async-start(bf16[8,2,64,375]{3,2,1,0:T(8,128)(2,1)} %copy.111), calls=%async_computation | async-start | bytes 1572864 | tf_op jit(solution)/shard_map/all_to_all | solution.py:87
  93.1 0.4 convolution_convert_fusion.1
  93.6 1.0 copy.128
  94.6 13.4 %all-to-all-done = bf16[8,2,64,375]{3,2,1,0:T(8,128)(2,1)S(1)} async-done(((bf16[8,2,64,375]{3,2,1,0:T(8,128)(2,1)}), bf16[8,2,64,375]{3,2,1,0:T(8,128)(2,1)S(1)}, u32[]{:S(2)}, u32[]{:S(2)}) %all-to-all-start) | async-done | bytes 768032 | tf_op jit(solution)/shard_map/all_to_all | solution.py:87
  108.0 4.2 %all-to-all-start.4 = ((bf16[8,2,64,375]{3,2,1,0:T(8,128)(2,1)}), bf16[8,2,64,375]{3,2,1,0:T(8,128)(2,1)}, u32[]{:S(2)}, u32[]{:S(2)}) async-start(bf16[8,2,64,375]{3,2,1,0:T(8,128)(2,1)} %copy.128), calls=%async_computation.4 | async-start | bytes 1572864 | tf_op jit(solution)/shard_map/all_to_all | solution.py:86
  112.2 5.5 %reduce-scatter.4.cloned.1.call-done = f32[375,8,128]{2,1,0:T(8,128)} async-done(((f32[1500,8,128]{2,1,0:T(8,128)}), f32[375,8,128]{2,1,0:T(8,128)}) %reduce-scatter.4.cloned.1.call-update) | async-done | bytes 1536016
  117.7 1.5 convert_element_type.77
  119.1 1.0 copy.124
  120.1 9.4 %all-to-all-done.4 = bf16[8,2,64,375]{3,2,1,0:T(8,128)(2,1)} async-done(((bf16[8,2,64,375]{3,2,1,0:T(8,128)(2,1)}), bf16[8,2,64,375]{3,2,1,0:T(8,128)(2,1)}, u32[]{:S(2)}, u32[]{:S(2)}) %all-to-all-start.4) | async-done | bytes 768032 | tf_op jit(solution)/shard_map/all_to_all | solution.py:86
  129.5 4.2 %all-to-all-start.3 = ((bf16[375,8,128]{2,0,1:T(8,128)(2,1)}), bf16[375,8,128]{2,0,1:T(8,128)(2,1)}, u32[]{:S(2)}, u32[]{:S(2)}) async-start(bf16[375,8,128]{2,0,1:T(8,128)(2,1)} %copy.124), calls=%async_computation.3 | async-start | bytes 1540096 | tf_op jit(solution)/shard_map/all_to_all | solution.py:63
  133.8 0.2 convert_reduce_fusion.2
  134.0 0.5 convert_multiply_fusion
  134.5 0.6 convolution_convert_fusion.4
  135.0 2.6 convolution_convert_fusion
  137.7 2.3 fusion.6
  140.0 12.0 %all-to-all-done.3 = bf16[375,8,128]{2,0,1:T(8,128)(2,1)} async-done(((bf16[375,8,128]{2,0,1:T(8,128)(2,1)}), bf16[375,8,128]{2,0,1:T(8,128)(2,1)}, u32[]{:S(2)}, u32[]{:S(2)}) %all-to-all-start.3) | async-done | bytes 768032 | tf_op jit(solution)/shard_map/all_to_all | solution.py:63
  152.0 1.5 copy.125
  153.5 0.6 fusion.5
  154.1 0.5 copy-done.1
  154.6 0.1 copy-done.3
  154.7 1.2 convolution_subtract_fusion
  156.0 32.5 %all-reduce.5.cloned.1.call-done = f32[16,64,64]{2,1,0:T(8,128)} async-done(((f32[16,64,64]{2,1,0:T(8,128)}), f32[16,64,64]{2,1,0:T(8,128)}) %all-reduce.5.cloned.1.call-update) | async-done | bytes 262160 | tf_op jit(solution)/shard_map/psum | solution.py:110
  188.5 1.3 copy.132
  189.8 0.9 reshape.171
  190.7 2.2 fusion.37
  193.0 0.6 dynamic-slice.2
  194.3 0.9 reshape.170
  195.1 70.8 %all-reduce.7.cloned.1.call-done = f32[32,4096]{1,0:T(8,128)} async-done(((f32[32,4096]{1,0:T(8,128)}), f32[32,4096]{1,0:T(8,128)}) %all-reduce.7.cloned.1.call-update) | async-done | bytes 524304
  265.9 1.5 constant_dynamic-slice_fusion
  (34 shorter events, 0.7 us)
Async XLA Ops:
  7.2 42.0 %copy-start = (bf16[2,375,1500]{2,0,1:T(2,128)(2,1)S(1)}, bf16[2,375,1500]{2,0,1:T(2,128)(2,1)}, u32[]{:S(2)}) copy-start(bf16[2,375,1500]{2,0,1:T(2,128)(2,1)} %param.11) | copy-start | bytes 6750004
  9.9 13.7 %all-to-all-start.2 = ((s32[8,1,2]{2,1,0:T(1,128)}), s32[8,1,2]{2,1,0:T(1,128)S(1)}, u32[]{:S(2)}, u32[]{:S(2)}) async-start(s32[8,1,2]{2,1,0:T(1,128)} %bitcast.18), calls=%async_computation.2 | async-start | bytes 8192 | tf_op jit(solution)/shard_map/all_to_all | solution.py:50
  23.6 25.5 %all-to-all-start.1 = ((bf16[8,2,64,375]{3,1,2,0:T(2,128)(2,1)}), bf16[8,2,64,375]{3,1,2,0:T(2,128)(2,1)S(1)}, u32[]{:S(2)}, u32[]{:S(2)}) async-start(bf16[8,2,64,375]{3,1,2,0:T(2,128)(2,1)} %copy.117), calls=%async_computation.1 | async-start | bytes 1572864 | tf_op jit(solution)/shard_map/all_to_all | solution.py:49
  29.4 88.3 %reduce-scatter.4.cloned.1.call-start = ((), (), s32[]{:S(2)}) async-start(), calls=%async_computation.8 | async-start | bytes 7680000
  60.7 0.7 copy-start.6
  60.7 27.4 %copy-start.4 = (bf16[4,64,375]{2,1,0:T(8,128)(2,1)S(1)}, bf16[4,64,375]{2,1,0:T(8,128)(2,1)}, u32[]{:S(2)}) copy-start(bf16[4,64,375]{2,1,0:T(8,128)(2,1)} %param.9) | copy-start | bytes 576004
  88.5 4.6 %copy-start.5 = (bf16[4,64,375]{2,1,0:T(8,128)(2,1)S(1)}, bf16[4,64,375]{2,1,0:T(8,128)(2,1)}, u32[]{:S(2)}) copy-start(bf16[4,64,375]{2,1,0:T(8,128)(2,1)} %param.8) | copy-start | bytes 576004
  89.6 18.4 %all-to-all-start = ((bf16[8,2,64,375]{3,2,1,0:T(8,128)(2,1)}), bf16[8,2,64,375]{3,2,1,0:T(8,128)(2,1)S(1)}, u32[]{:S(2)}, u32[]{:S(2)}) async-start(bf16[8,2,64,375]{3,2,1,0:T(8,128)(2,1)} %copy.111), calls=%async_computation | async-start | bytes 1572864 | tf_op jit(solution)/shard_map/all_to_all | solution.py:87
  108.0 21.6 %all-to-all-start.4 = ((bf16[8,2,64,375]{3,2,1,0:T(8,128)(2,1)}), bf16[8,2,64,375]{3,2,1,0:T(8,128)(2,1)}, u32[]{:S(2)}, u32[]{:S(2)}) async-start(bf16[8,2,64,375]{3,2,1,0:T(8,128)(2,1)} %copy.128), calls=%async_computation.4 | async-start | bytes 1572864 | tf_op jit(solution)/shard_map/all_to_all | solution.py:86
  119.1 14.9 %copy-start.7 = (f32[375]{0:T(512)S(1)}, f32[375]{0:T(512)}, u32[]{:S(2)}) copy-start(f32[375]{0:T(512)} %param.10) | copy-start | bytes 4504
  129.5 22.4 %all-to-all-start.3 = ((bf16[375,8,128]{2,0,1:T(8,128)(2,1)}), bf16[375,8,128]{2,0,1:T(8,128)(2,1)}, u32[]{:S(2)}, u32[]{:S(2)}) async-start(bf16[375,8,128]{2,0,1:T(8,128)(2,1)} %copy.124), calls=%async_computation.3 | async-start | bytes 1540096 | tf_op jit(solution)/shard_map/all_to_all | solution.py:63
  133.7 54.8 %all-reduce.5.cloned.1.call-start = ((), (), s32[]{:S(2)}) async-start(), calls=%async_computation.6 | async-start | bytes 1048576 | tf_op jit(solution)/shard_map/psum | solution.py:110
  153.5 1.1 copy-start.1
  153.5 1.3 copy-start.3
  156.0 109.9 %all-reduce.7.cloned.1.call-start = ((), (), s32[]{:S(2)}) async-start(), calls=%async_computation.7 | async-start | bytes 1048576
  188.5 4.5 %copy-start.8 = (u32[32]{0:T(128)S(1)}, u32[32]{0:T(128)}, u32[]{:S(2)}) copy-start(u32[32]{0:T(128)} %constant.69) | copy-start | bytes 388
  188.5 5.7 %copy-start.2 = (f32[16,64,64]{2,1,0:T(8,128)S(1)}, f32[16,64,64]{2,1,0:T(8,128)}, u32[]{:S(2)}) copy-start(f32[16,64,64]{2,1,0:T(8,128)} %all-reduce.5.cloned.1.call-done) | copy-start | bytes 786436
Sparse Core Ops, SparseCore 0:
  60.9 56.7 reduce-scatter.3
  156.1 32.3 all-reduce.4
  193.1 72.7 all-reduce.6
where the time goes:
time: 275 us; the launch traced here: 274 us
  waiting for transfers between devices  163 us (59%)
  blocking collectives  26.1 us (9%)
  starting transfers between devices  25.2 us (9%)
  local copies, waits for them, and re-layouts  22.1 us (8%)
  matrix products  18.5 us (7%)
  between operations  14.6 us (5%)
  other arithmetic  4.08 us (1%)
    unnamed x5, waiting for transfers between devices  76.3 us
    psum x1, waiting for transfers between devices, per_device(): kernel_block = lax.psum(2.0 * exchange_term - direct, 'ga')  32.5 us
    all_gather x1, blocking collectives, per_device(): lax.all_gather(pairs, 'ka', axis=0, tiled=True).reshape(n_ka, pair_rows, 3)  26.1 us
    all_to_all x1, waiting for transfers between devices, per_device(): lax.all_to_all(send_x, 'ka', split_axis=0, concat_axis=0, tiled=True)  19.6 us
    all_to_all x1, waiting for transfers between devices, per_device(): lax.all_to_all(send_p, 'ka', split_axis=0, concat_axis=0, tiled=True)  13.4 us
    all_to_all x1, waiting for transfers between devices, per_device(): lax.all_to_all(half_rows, 'ka', split_axis=1, concat_axis=1, tiled=True)  12 us
    all_to_all x1, waiting for transfers between devices, per_device(): lax.all_to_all(send_y, 'ka', split_axis=0, concat_axis=0, tiled=True)  9.42 us
    all_to_all x1, starting transfers between devices, per_device(): lax.all_to_all(send_q, 'ka', split_axis=0, concat_axis=0, tiled=True)  7.31 us
  transfers between devices with their start and end apart: 8, of which 8 were waited for; matrix products, arithmetic and copies ran while one was open for 7% of the time, Pallas kernels for 0%

commit v1 on v0

--- a/solution.py
+++ b/solution.py
@@ -107,7 +107,7 @@
     exchange_term = jnp.einsum(
         "jig,jhg->jih", weighted, pp_rows.astype(jnp.float32), precision=lax.Precision.HIGHEST
     )
-    kernel_block = lax.psum(2.0 * exchange_term - direct, "ga")
+    kernel_block = jnp.sum(lax.all_gather(2.0 * exchange_term - direct, "ga"), axis=0)
     blocks = kernel_block.reshape(pair_rows, transitions * transitions)
     flipped = jnp.transpose(kernel_block, (0, 2, 1)).reshape(pair_rows, transitions * transitions)
     selector = (partner[:, None] == jnp.arange(lax.axis_size("ka") * per_dev)[None, :]).astype(

time: 275 us -> 265 us (0.964)
  waiting for transfers between devices: 163 us -> 152 us
    psum x1 -> x0, waiting for transfers between devices: 32.5 us -> none  [per_device(): kernel_block = lax.psum(2.0 * exchange_term - direct, 'ga')]
    all_gather x0 -> x1, waiting for transfers between devices: none -> 21.7 us  [per_device(): lax.all_gather(2.0 * exchange_term - direct, 'ga')]
  transfers between devices with their start and end apart: 8 -> 8, of which waited for: 8 -> 8; matrix products, arithmetic and copies ran while one was open for 7% -> 8% of each run, Pallas kernels for 0% -> 0%
where the time goes in v1:
time: 265 us; the launch traced here: 264 us
  waiting for transfers between devices  152 us (57%)
  blocking collectives  26.1 us (10%)
  starting transfers between devices  25.2 us (10%)
  local copies, waits for them, and re-layouts  21.1 us (8%)
  matrix products  18.6 us (7%)
  between operations  14.6 us (6%)
  other arithmetic  5.97 us (2%)
    unnamed x5, waiting for transfers between devices  76.1 us
    all_gather x1, blocking collectives, per_device(): lax.all_gather(pairs, 'ka', axis=0, tiled=True).reshape(n_ka, pair_rows, 3)  26.1 us
    all_gather x1, waiting for transfers between devices, per_device(): lax.all_gather(2.0 * exchange_term - direct, 'ga')  21.7 us
    all_to_all x1, waiting for transfers between devices, per_device(): lax.all_to_all(send_x, 'ka', split_axis=0, concat_axis=0, tiled=True)  19.6 us
    all_to_all x1, waiting for transfers between devices, per_device(): lax.all_to_all(send_p, 'ka', split_axis=0, concat_axis=0, tiled=True)  13.4 us
    all_to_all x1, waiting for transfers between devices, per_device(): lax.all_to_all(half_rows, 'ka', split_axis=1, concat_axis=1, tiled=True)  12 us
    all_to_all x1, waiting for transfers between devices, per_device(): lax.all_to_all(send_y, 'ka', split_axis=0, concat_axis=0, tiled=True)  9.44 us
    all_to_all x1, starting transfers between devices, per_device(): lax.all_to_all(send_q, 'ka', split_axis=0, concat_axis=0, tiled=True)  7.31 us
  transfers between devices with their start and end apart: 8, of which 8 were waited for; matrix products, arithmetic and copies ran while one was open for 8% of the time, Pallas kernels for 0%

profile of v1, /device:TPU:0, one launch (start us, length us, event | category | flops | bytes accessed | tf_op | source)
XLA Modules:
  0.0 263.9 jit_solution(3420602591104036494)
XLA Ops:
  7.2 0.9 slice_bitcast_fusion.1
  8.1 0.8 select_reduce_fusion
  8.9 0.2 convert_reduce_fusion.1
  9.2 0.7 all_to_all.20
  9.9 7.3 %all-to-all-start.2 = ((s32[8,1,2]{2,1,0:T(1,128)}), s32[8,1,2]{2,1,0:T(1,128)S(1)}, u32[]{:S(2)}, u32[]{:S(2)}) async-start(s32[8,1,2]{2,1,0:T(1,128)} %bitcast.18), calls=%async_computation.2 | async-start | bytes 8192 | tf_op jit(solution)/shard_map/all_to_all | solution.py:50
  17.2 2.5 convolution_convert_fusion.3
  19.7 2.2 reshape.166
  21.9 1.5 copy.117
  23.4 0.2 all-to-all-done.2
  23.6 5.8 %all-to-all-start.1 = ((bf16[8,2,64,375]{3,1,2,0:T(2,128)(2,1)}), bf16[8,2,64,375]{3,1,2,0:T(2,128)(2,1)S(1)}, u32[]{:S(2)}, u32[]{:S(2)}) async-start(bf16[8,2,64,375]{3,1,2,0:T(2,128)(2,1)} %copy.117), calls=%async_computation.1 | async-start | bytes 1572864 | tf_op jit(solution)/shard_map/all_to_all | solution.py:49
  29.5 19.6 %all-to-all-done.1 = bf16[8,2,64,375]{3,1,2,0:T(2,128)(2,1)S(1)} async-done(((bf16[8,2,64,375]{3,1,2,0:T(2,128)(2,1)}), bf16[8,2,64,375]{3,1,2,0:T(2,128)(2,1)S(1)}, u32[]{:S(2)}, u32[]{:S(2)}) %all-to-all-start.1) | async-done | bytes 768032 | tf_op jit(solution)/shard_map/all_to_all | solution.py:49
  49.2 5.0 %fusion = f32[8,2,64,1500,1]{3,2,4,1,0:T(8,128)} fusion(bf16[2,375,1500,1,1]{2,0,1,4,3:T(2,128)(2,1)S(1)} %bitcast.73, bf16[8,2,2]{2,1,0:T(2,128)(2,1)S(1)} %compare_convert_fusion, bf16[8,2,64,375]{3,2,1,0:T(8,128)(2,1)S(1)} %copy.118), kind=kOutput, calls=%fused_computation | convolution fusion | flops 2304768000 | bytes 9162064 | tf_op jit(solution)/shard_map/ncsig,sgh->hnci/dot_general | solution.py:54
  54.3 6.5 %copy.123 = f32[1500,8,128]{2,1,0:T(8,128)} copy(f32[1500,8,128]{0,2,1:T(8,128)} %bitcast.74) | data formatting | bytes 12288000 | tf_op jit(solution)/shard_map/reshape | solution.py:58
  60.8 0.7 copy-done.5
  61.5 26.1 %all-gather.1 = s32[8,16,3]{1,2,0:T(4,128)S(1)} all-gather(s32[1,16,3]{1,2,0:T(4,128)S(1)} %bitcast.83), channel_id=1, replica_groups=mesh['ka'=8,'ga'=4] {'ka'}, dimensions={0}, use_global_device_ids=true | all-gather | bytes 1728 | tf_op jit(solution)/shard_map/all_gather | solution.py:68
  87.6 0.3 convert_reduce_fusion
  88.2 0.4 convolution_convert_fusion.5
  88.6 1.0 copy.111
  89.6 3.5 %all-to-all-start = ((bf16[8,2,64,375]{3,2,1,0:T(8,128)(2,1)}), bf16[8,2,64,375]{3,2,1,0:T(8,128)(2,1)S(1)}, u32[]{:S(2)}, u32[]{:S(2)}) async-start(bf16[8,2,64,375]{3,2,1,0:T(8,128)(2,1)} %copy.111), calls=%async_computation | async-start | bytes 1572864 | tf_op jit(solution)/shard_map/all_to_all | solution.py:87
  93.2 0.4 convolution_convert_fusion.1
  93.6 1.0 copy.128
  94.6 13.4 %all-to-all-done = bf16[8,2,64,375]{3,2,1,0:T(8,128)(2,1)S(1)} async-done(((bf16[8,2,64,375]{3,2,1,0:T(8,128)(2,1)}), bf16[8,2,64,375]{3,2,1,0:T(8,128)(2,1)S(1)}, u32[]{:S(2)}, u32[]{:S(2)}) %all-to-all-start) | async-done | bytes 768032 | tf_op jit(solution)/shard_map/all_to_all | solution.py:87
  108.0 4.2 %all-to-all-start.4 = ((bf16[8,2,64,375]{3,2,1,0:T(8,128)(2,1)}), bf16[8,2,64,375]{3,2,1,0:T(8,128)(2,1)}, u32[]{:S(2)}, u32[]{:S(2)}) async-start(bf16[8,2,64,375]{3,2,1,0:T(8,128)(2,1)} %copy.128), calls=%async_computation.4 | async-start | bytes 1572864 | tf_op jit(solution)/shard_map/all_to_all | solution.py:86
  112.3 5.4 %reduce-scatter.4.cloned.1.call-done = f32[375,8,128]{2,1,0:T(8,128)} async-done(((f32[1500,8,128]{2,1,0:T(8,128)}), f32[375,8,128]{2,1,0:T(8,128)}) %reduce-scatter.4.cloned.1.call-update) | async-done | bytes 1536016
  117.7 1.5 convert_element_type.77
  119.2 1.0 copy.124
  120.2 9.4 %all-to-all-done.4 = bf16[8,2,64,375]{3,2,1,0:T(8,128)(2,1)} async-done(((bf16[8,2,64,375]{3,2,1,0:T(8,128)(2,1)}), bf16[8,2,64,375]{3,2,1,0:T(8,128)(2,1)}, u32[]{:S(2)}, u32[]{:S(2)}) %all-to-all-start.4) | async-done | bytes 768032 | tf_op jit(solution)/shard_map/all_to_all | solution.py:86
  129.6 4.2 %all-to-all-start.3 = ((bf16[375,8,128]{2,0,1:T(8,128)(2,1)}), bf16[375,8,128]{2,0,1:T(8,128)(2,1)}, u32[]{:S(2)}, u32[]{:S(2)}) async-start(bf16[375,8,128]{2,0,1:T(8,128)(2,1)} %copy.124), calls=%async_computation.3 | async-start | bytes 1540096 | tf_op jit(solution)/shard_map/all_to_all | solution.py:63
  133.9 0.2 convert_reduce_fusion.2
  134.1 0.5 convert_multiply_fusion
  134.5 0.6 convolution_convert_fusion.4
  135.1 2.6 convolution_convert_fusion
  137.7 2.3 fusion.6
  140.1 12.0 %all-to-all-done.3 = bf16[375,8,128]{2,0,1:T(8,128)(2,1)} async-done(((bf16[375,8,128]{2,0,1:T(8,128)(2,1)}), bf16[375,8,128]{2,0,1:T(8,128)(2,1)}, u32[]{:S(2)}, u32[]{:S(2)}) %all-to-all-start.3) | async-done | bytes 768032 | tf_op jit(solution)/shard_map/all_to_all | solution.py:63
  152.0 1.5 copy.125
  153.5 0.6 fusion.5
  154.1 0.5 copy-done.1
  154.7 0.1 copy-done.2
  154.8 1.2 convolution_subtract_fusion
  156.1 21.7 %all-gather.4.cloned.1.call-done = f32[64,64,64]{2,1,0:T(8,128)} async-done(((f32[16,64,64]{2,1,0:T(8,128)}), f32[64,64,64]{2,1,0:T(8,128)}) %all-gather.4.cloned.1.call-update) | async-done | bytes 1048592 | tf_op jit(solution)/shard_map/all_gather | solution.py:110
  177.8 1.9 reduce_sum.62
  179.7 0.2 copy.132
  179.9 0.9 reshape.171
  180.8 2.2 fusion.37
  183.0 0.6 dynamic-slice.2
  184.3 0.9 reshape.170
  185.2 70.7 %all-reduce.4.cloned.1.call-done = f32[32,4096]{1,0:T(8,128)} async-done(((f32[32,4096]{1,0:T(8,128)}), f32[32,4096]{1,0:T(8,128)}) %all-reduce.4.cloned.1.call-update) | async-done | bytes 524304
  255.8 1.5 constant_dynamic-slice_fusion
  (33 shorter events, 0.8 us)
Async XLA Ops:
  7.2 42.1 %copy-start = (bf16[2,375,1500]{2,0,1:T(2,128)(2,1)S(1)}, bf16[2,375,1500]{2,0,1:T(2,128)(2,1)}, u32[]{:S(2)}) copy-start(bf16[2,375,1500]{2,0,1:T(2,128)(2,1)} %param.11) | copy-start | bytes 6750004
  9.9 13.7 %all-to-all-start.2 = ((s32[8,1,2]{2,1,0:T(1,128)}), s32[8,1,2]{2,1,0:T(1,128)S(1)}, u32[]{:S(2)}, u32[]{:S(2)}) async-start(s32[8,1,2]{2,1,0:T(1,128)} %bitcast.18), calls=%async_computation.2 | async-start | bytes 8192 | tf_op jit(solution)/shard_map/all_to_all | solution.py:50
  23.6 25.5 %all-to-all-start.1 = ((bf16[8,2,64,375]{3,1,2,0:T(2,128)(2,1)}), bf16[8,2,64,375]{3,1,2,0:T(2,128)(2,1)S(1)}, u32[]{:S(2)}, u32[]{:S(2)}) async-start(bf16[8,2,64,375]{3,1,2,0:T(2,128)(2,1)} %copy.117), calls=%async_computation.1 | async-start | bytes 1572864 | tf_op jit(solution)/shard_map/all_to_all | solution.py:49
  29.4 88.3 %reduce-scatter.4.cloned.1.call-start = ((), (), s32[]{:S(2)}) async-start(), calls=%async_computation.8 | async-start | bytes 7680000
  60.8 0.7 copy-start.5
  60.8 27.4 %copy-start.3 = (bf16[4,64,375]{2,1,0:T(8,128)(2,1)S(1)}, bf16[4,64,375]{2,1,0:T(8,128)(2,1)}, u32[]{:S(2)}) copy-start(bf16[4,64,375]{2,1,0:T(8,128)(2,1)} %param.9) | copy-start | bytes 576004
  88.6 4.6 %copy-start.4 = (bf16[4,64,375]{2,1,0:T(8,128)(2,1)S(1)}, bf16[4,64,375]{2,1,0:T(8,128)(2,1)}, u32[]{:S(2)}) copy-start(bf16[4,64,375]{2,1,0:T(8,128)(2,1)} %param.8) | copy-start | bytes 576004
  89.6 18.4 %all-to-all-start = ((bf16[8,2,64,375]{3,2,1,0:T(8,128)(2,1)}), bf16[8,2,64,375]{3,2,1,0:T(8,128)(2,1)S(1)}, u32[]{:S(2)}, u32[]{:S(2)}) async-start(bf16[8,2,64,375]{3,2,1,0:T(8,128)(2,1)} %copy.111), calls=%async_computation | async-start | bytes 1572864 | tf_op jit(solution)/shard_map/all_to_all | solution.py:87
  108.0 21.6 %all-to-all-start.4 = ((bf16[8,2,64,375]{3,2,1,0:T(8,128)(2,1)}), bf16[8,2,64,375]{3,2,1,0:T(8,128)(2,1)}, u32[]{:S(2)}, u32[]{:S(2)}) async-start(bf16[8,2,64,375]{3,2,1,0:T(8,128)(2,1)} %copy.128), calls=%async_computation.4 | async-start | bytes 1572864 | tf_op jit(solution)/shard_map/all_to_all | solution.py:86
  119.2 14.9 %copy-start.6 = (f32[375]{0:T(512)S(1)}, f32[375]{0:T(512)}, u32[]{:S(2)}) copy-start(f32[375]{0:T(512)} %param.10) | copy-start | bytes 4504
  129.6 22.4 %all-to-all-start.3 = ((bf16[375,8,128]{2,0,1:T(8,128)(2,1)}), bf16[375,8,128]{2,0,1:T(8,128)(2,1)}, u32[]{:S(2)}, u32[]{:S(2)}) async-start(bf16[375,8,128]{2,0,1:T(8,128)(2,1)} %copy.124), calls=%async_computation.3 | async-start | bytes 1540096 | tf_op jit(solution)/shard_map/all_to_all | solution.py:63
  133.8 44.0 %all-gather.4.cloned.1.call-start = ((), (), s32[]{:S(2)}) async-start(), calls=%async_computation.6 | async-start | bytes 2621440 | tf_op jit(solution)/shard_map/all_gather | solution.py:110
  153.5 1.1 copy-start.1
  153.5 1.3 copy-start.2
  156.1 99.8 %all-reduce.4.cloned.1.call-start = ((), (), s32[]{:S(2)}) async-start(), calls=%async_computation.7 | async-start | bytes 1048576
  179.7 3.4 %copy-start.7 = (u32[32]{0:T(128)S(1)}, u32[32]{0:T(128)}, u32[]{:S(2)}) copy-start(u32[32]{0:T(128)} %constant.71) | copy-start | bytes 388
Sparse Core Ops, SparseCore 0:
  60.9 56.7 reduce-scatter.3
  156.2 21.5 all-gather.3
  183.1 72.6 all-reduce.3
